TPU v7x, 256 devices: a whole 4x4x8 slice. The times are simulated.
256 devices in a mesh: gx: 4 (over x), gy: 4 (over y), gz: 16 (over z, core).
Axes of the slice: x: 4, y: 4, z: 8, core: 2. Of those that a mesh axis runs over, the one named last changes fastest.
Arguments:
- log_probs: float32 [65536, 1024], P(('gx', 'gy', 'gz')), may hold values from -2 to 0
- ref_log_probs: float32 [65536, 1024], P(('gx', 'gy', 'gz')), may hold values from -2 to 0
- rewards: float32 [65536, 128], P(('gx', 'gy', 'gz')), may hold values from -6 to 6
- destination: int32 [65536], P(('gx', 'gy', 'gz')), may hold values from 0 to 65535, as said below
- lengths: int32 [65536], P(('gx', 'gy', 'gz')), may hold values from 1 to 1024
- mixing: float32 [128], replicated, may hold values from -0.5 to 0.5
Outputs:
- token_loss: float32 [65536, 1024], P(('gx', 'gy', 'gz'))
- advantages: float32 [65536, 128], P(('gx', 'gy', 'gz'))
Inputs may be any that keep to these rules, and one draw needn't show every extreme that they name: A permutation. Rows are numbered along gx+gy+gz, 256 a device. Moving each row first to the gx index of its destination device, then to its gy index, then to its gz index, every device holds exactly 256 rows after each move, and at the three moves one device sends at most 128, 128 and 32 rows to one index, bounds reached in every draw.
All inputs are finite; a program needn't handle non-finite values.
Results may differ from a plain program's by a relative error of at most 0.0003.
Values sent between devices are 32-bit elements; how exact they have to be, the bound alone decides.
A program may use at most 64 MiB of HBM per device.

v0:
```python
import jax
import jax.numpy as jnp
from jax import lax
from jax.sharding import PartitionSpec as P

GROUP = 16


beta = 0.2


def in_one_piece(arrays, axis, split_dim, concat_dim, along):
    ends, at = ([], 0)
    for a in arrays[:-1]:
        at += a.shape[along]
        ends.append(at)
    both = jnp.concatenate(arrays, axis=along)
    return tuple(
        jnp.split(
            lax.all_to_all(both, axis, split_axis=split_dim, concat_axis=concat_dim, tiled=True),
            ends,
            axis=along,
        )
    )


def pack_rows(payload, target, fanout, capacity):
    local_rows = target.shape[0]
    onehot = (target[:, None] == jnp.arange(fanout, dtype=jnp.int32)[None, :]).astype(jnp.int32)
    ranking = jnp.sum((jnp.cumsum(onehot, axis=0) - onehot) * onehot, axis=1)
    bucket_slot = target * capacity + ranking
    source = (
        jnp.zeros((fanout * capacity,), jnp.int32)
        .at[bucket_slot]
        .set(jnp.arange(local_rows, dtype=jnp.int32))
    )
    filled = jnp.zeros((fanout * capacity,), jnp.int32).at[bucket_slot].set(1) > 0
    packed = []
    for number, member in enumerate(payload):
        empty_value = -1.0 if number == len(payload) - 1 else 0.0
        picked = jnp.where(filled[:, None], member[source], jnp.float32(empty_value))
        packed.append(picked.reshape(fanout, capacity, member.shape[1]))
    return tuple(packed)


def route_step(payload, local_rows, fanout, stride):
    target = payload[-1][:, 0].astype(jnp.int32) // local_rows // stride % fanout
    return pack_rows(payload, target, fanout, 2 * local_rows // fanout)


def flatten(payload):
    return tuple((member.reshape(-1, member.shape[-1]) for member in payload))


def settle(payload, local_rows, landing):
    source = (
        jnp.zeros((local_rows,), jnp.int32)
        .at[landing]
        .set(jnp.arange(landing.shape[0], dtype=jnp.int32), mode="drop")
    )
    return tuple((member[source] for member in payload))


def compact(payload, local_rows):
    present = payload[-1][:, 0] >= 0.0
    landing = jnp.where(present, jnp.cumsum(present.astype(jnp.int32)) - 1, local_rows)
    return settle(payload, local_rows, landing)


def finish(payload, local_rows):
    present = payload[-1][:, 0] >= 0.0
    landing = jnp.where(present, payload[-1][:, 0].astype(jnp.int32) % local_rows, local_rows)
    return settle(payload, local_rows, landing)


def losses(policy, older, weight, reaches):
    log_gap = older - policy
    penalty = jnp.exp(log_gap) - log_gap - 1.0
    inside = jnp.arange(policy.shape[1], dtype=jnp.int32)[None, :] < reaches[:, None]
    return jnp.where(inside, beta * penalty - weight[:, None] * policy, jnp.float32(0.0))


def normalize(judged, mixing):
    local_rows = judged.shape[0]
    grouped = judged.reshape(local_rows // GROUP, GROUP, judged.shape[1])
    centre = jnp.mean(grouped, axis=1, keepdims=True)
    deviation = grouped - centre
    spread = jnp.mean(deviation * deviation, axis=1, keepdims=True)
    advantages = (deviation / jnp.sqrt(spread + 1.0)).reshape(local_rows, judged.shape[1])
    weight = jnp.dot(advantages, mixing, precision=lax.Precision.HIGHEST)
    return (advantages, weight)


def on_device(log_probs, ref_log_probs, rewards, destination, lengths, mixing):
    local_rows = log_probs.shape[0]
    size_x = lax.axis_size("gx")
    size_y = lax.axis_size("gy")
    size_z = lax.axis_size("gz")
    header = jnp.stack([destination.astype(jnp.float32), lengths.astype(jnp.float32)], axis=1)
    policy, older, judged, header = route_step(
        (log_probs, ref_log_probs, rewards, header), local_rows, size_x, size_y * size_z
    )
    policy, older, judged, header = compact(
        flatten(in_one_piece((policy, older, judged, header), "gx", 0, 0, 2)), local_rows
    )
    policy, older, judged, header = route_step(
        (policy, older, judged, header), local_rows, size_y, size_z
    )
    policy, older, judged, header = compact(
        flatten(
            (
                lax.all_to_all(policy, "gy", split_axis=0, concat_axis=0, tiled=True),
                lax.all_to_all(older, "gy", split_axis=0, concat_axis=0, tiled=True),
                lax.all_to_all(judged, "gy", split_axis=0, concat_axis=0, tiled=True),
                lax.all_to_all(header, "gy", split_axis=0, concat_axis=0, tiled=True),
            )
        ),
        local_rows,
    )
    policy, older, judged, header = route_step(
        (policy, older, judged, header), local_rows, size_z, 1
    )
    policy, older, judged, header = finish(
        flatten(in_one_piece((policy, older, judged, header), "gz", 0, 0, 2)), local_rows
    )
    advantages, weight = normalize(judged, mixing)
    token_loss = losses(policy, older, weight, header[:, 1].astype(jnp.int32))
    return (token_loss, advantages)


def solution(mesh):
    in_specs = (
        P(("gx", "gy", "gz"), None),
        P(("gx", "gy", "gz"), None),
        P(("gx", "gy", "gz"), None),
        P(("gx", "gy", "gz")),
        P(("gx", "gy", "gz")),
        P(),
    )
    out_specs = (P(("gx", "gy", "gz"), None), P(("gx", "gy", "gz"), None))
    return jax.shard_map(
        on_device, mesh=mesh, in_specs=in_specs, out_specs=out_specs, check_vma=False
    )
```

profile of v0, /device:TPU:1, one launch (start us, length us, event | category | flops | bytes accessed | tf_op | source)
XLA Modules:
  0.0 331.8 jit_solution(14199186585453830019)
XLA Ops:
  9.2 1.9 gather_fusion.1
  13.0 1.9 gather_fusion
  14.9 1.9 copy.27
  16.8 2.6 broadcast_select_fusion.5
  19.6 55.4 %all_to_all.30 = f32[4,128,2178]{1,2,0:T(8,128)S(1)} all-to-all(f32[4,128,2178]{1,2,0:T(8,128)S(1)} %pad_maximum_fusion.1), channel_id=1, replica_groups=mesh['gx'=4,'gy'=4,'gz'=16] {'gx'}, dimensions={0} | all-to-all | bytes 8921088 | tf_op jit(solution)/shard_map/all_to_all | solution.py:20
  75.1 2.0 copy-done.5
  78.4 2.4 scatter_custom_fusion.2
  88.4 4.2 %all-to-all-start.1 = ((f32[4,128,2]{1,2,0:T(2,128)}), f32[4,128,2]{1,2,0:T(2,128)S(1)}, u32[]{:S(2)}, u32[]{:S(2)}) async-start(f32[4,128,2]{1,2,0:T(2,128)} %broadcast_select_fusion.10), calls=%async_computation.1 | async-start | bytes 8192 | tf_op jit(solution)/shard_map/all_to_all | solution.py:115
  94.6 4.5 %fusion.56 = (f32[4,128,1024]{1,2,0:T(8,128)}, f32[4,128,1024]{1,2,0:T(8,128)}) fusion(f32[4,128,2178]{1,2,0:T(8,128)} %copy-done.5), kind=kLoop, calls=%fused_computation.192 | loop fusion | bytes 8388608 | tf_op jit(solution)/shard_map/split | solution.py:19
  99.9 1.9 copy.42
  102.9 1.9 gather_fusion.8
  106.7 1.9 copy.45
  109.7 1.9 gather_fusion.12
  113.5 4.2 %all-to-all-start.4 = ((f32[4,128,128]{1,2,0:T(8,128)}), f32[4,128,128]{1,2,0:T(8,128)S(1)}, u32[]{:S(2)}, u32[]{:S(2)}) async-start(f32[4,128,128]{1,2,0:T(8,128)} %broadcast_select_fusion.8), calls=%async_computation.4 | async-start | bytes 524288 | tf_op jit(solution)/shard_map/all_to_all | solution.py:114
  117.7 4.5 %broadcast_select_fusion.3 = (f32[4,128,1024]{1,2,0:T(8,128)}, f32[4,128,1024]{1,2,0:T(8,128)}) fusion(f32[4,128,1024]{1,2,0:T(8,128)} %copy.43, pred[4,128]{1,0:T(4,128)(4,1)S(1)} %compare_bitcast_fusion, f32[4,128,1024]{1,2,0:T(8,128)} %copy.46), kind=kLoop, calls=%fused_computation.43 | loop fusion | flops 1048576 | bytes 8389120 | tf_op jit(solution)/shard_map/jit(_where)/select_n | solution.py:41
  123.2 3.6 %all-to-all-start.2 = ((f32[4,128,1024]{1,2,0:T(8,128)}), f32[4,128,1024]{1,2,0:T(8,128)S(1)}, u32[]{:S(2)}, u32[]{:S(2)}) async-start(f32[4,128,1024]{1,2,0:T(8,128)} %get-tuple-element.18), calls=%async_computation.2 | async-start | bytes 4194304 | tf_op jit(solution)/shard_map/all_to_all | solution.py:112
  128.1 2.4 scatter_custom_fusion.5
  131.5 17.8 %all-to-all-done.2 = f32[4,128,1024]{1,2,0:T(8,128)S(1)} async-done(((f32[4,128,1024]{1,2,0:T(8,128)}), f32[4,128,1024]{1,2,0:T(8,128)S(1)}, u32[]{:S(2)}, u32[]{:S(2)}) %all-to-all-start.2) | async-done | bytes 2097184 | tf_op jit(solution)/shard_map/all_to_all | solution.py:112
  150.6 4.4 %all-to-all-start.3 = ((f32[4,128,1024]{1,2,0:T(8,128)}), f32[4,128,1024]{1,2,0:T(8,128)}, u32[]{:S(2)}, u32[]{:S(2)}) async-start(f32[4,128,1024]{1,2,0:T(8,128)} %get-tuple-element.19), calls=%async_computation.3 | async-start | bytes 4194304 | tf_op jit(solution)/shard_map/all_to_all | solution.py:113
  163.3 1.9 copy.44
  166.3 10.4 %all-to-all-done.3 = f32[4,128,1024]{1,2,0:T(8,128)} async-done(((f32[4,128,1024]{1,2,0:T(8,128)}), f32[4,128,1024]{1,2,0:T(8,128)}, u32[]{:S(2)}, u32[]{:S(2)}) %all-to-all-start.3) | async-done | bytes 2097184 | tf_op jit(solution)/shard_map/all_to_all | solution.py:113
  176.7 2.9 copy.47
  179.6 3.2 gather_fusion.13
  182.8 2.7 gather_fusion.14
  185.4 2.7 gather_fusion.10
  188.2 2.0 broadcast_select_fusion.1
  190.6 121.0 %all_to_all.31 = f32[16,32,2178]{2,1,0:T(8,128)S(1)} all-to-all(f32[16,32,2178]{2,1,0:T(8,128)S(1)} %pad_maximum_fusion), channel_id=1, replica_groups=mesh['gx'=4,'gy'=4,'gz'=16] {'gz'}, dimensions={0} | all-to-all | bytes 8921088 | tf_op jit(solution)/shard_map/all_to_all | solution.py:20
  311.6 2.1 copy-done.4
  314.0 2.4 scatter_custom_fusion.8
  317.8 4.1 %fusion.55 = (f32[16,32,1024]{2,1,0:T(8,128)S(1)}, f32[16,32,1024]{2,1,0:T(8,128)}) fusion(f32[16,32,2178]{2,1,0:T(8,128)} %copy-done.4), kind=kLoop, calls=%fused_computation.191 | loop fusion | bytes 8388608 | tf_op jit(solution)/shard_map/split | solution.py:19
  321.9 4.1 %gather_fusion.22 = f32[256,1024]{1,0:T(8,128)} fusion(f32[512,1024]{1,0:T(8,128)} %bitcast.126, s32[1024]{0:T(1024)S(1)} %pad_clamp_fusion), kind=kCustom, calls=%fused_computation.22 | custom fusion | bytes 2098176 | tf_op jit(solution)/shard_map/gather | solution.py:61
  326.0 2.1 gather_fusion.21
  (155 shorter events, 47.5 us)
Async XLA Ops:
  0.6 8.6 %copy-start = (f32[256,1024]{1,0:T(8,128)S(1)}, f32[256,1024]{1,0:T(8,128)}, u32[]{:S(2)}) copy-start(f32[256,1024]{1,0:T(8,128)} %param.7) | copy-start | bytes 3145732
  0.6 7.3 %copy-start.3 = (f32[256,128]{1,0:T(8,128)S(1)}, f32[256,128]{1,0:T(8,128)}, u32[]{:S(2)}) copy-start(f32[256,128]{1,0:T(8,128)} %param.8) | copy-start | bytes 393220
  11.2 1.8 copy-start.2
  75.1 2.1 copy-start.5
  81.6 11.0 %slice-start.1 = ((f32[4,128,2178]{1,2,0:T(8,128)}), f32[4,128,128]{1,2,0:T(8,128)S(1)}, s32[]{:S(2)}) async-start(f32[4,128,2178]{1,2,0:T(8,128)} %copy-done.5), calls=%async_computation.7 | async-start | bytes 524288 | tf_op jit(solution)/shard_map/split | solution.py:19
  88.4 25.0 %all-to-all-start.1 = ((f32[4,128,2]{1,2,0:T(2,128)}), f32[4,128,2]{1,2,0:T(2,128)S(1)}, u32[]{:S(2)}, u32[]{:S(2)}) async-start(f32[4,128,2]{1,2,0:T(2,128)} %broadcast_select_fusion.10), calls=%async_computation.1 | async-start | bytes 8192 | tf_op jit(solution)/shard_map/all_to_all | solution.py:115
  113.5 9.8 %all-to-all-start.4 = ((f32[4,128,128]{1,2,0:T(8,128)}), f32[4,128,128]{1,2,0:T(8,128)S(1)}, u32[]{:S(2)}, u32[]{:S(2)}) async-start(f32[4,128,128]{1,2,0:T(8,128)} %broadcast_select_fusion.8), calls=%async_computation.4 | async-start | bytes 524288 | tf_op jit(solution)/shard_map/all_to_all | solution.py:114
  123.2 26.0 %all-to-all-start.2 = ((f32[4,128,1024]{1,2,0:T(8,128)}), f32[4,128,1024]{1,2,0:T(8,128)S(1)}, u32[]{:S(2)}, u32[]{:S(2)}) async-start(f32[4,128,1024]{1,2,0:T(8,128)} %get-tuple-element.18), calls=%async_computation.2 | async-start | bytes 4194304 | tf_op jit(solution)/shard_map/all_to_all | solution.py:112
  149.3 1.3 copy-start.7
  150.6 26.1 %all-to-all-start.3 = ((f32[4,128,1024]{1,2,0:T(8,128)}), f32[4,128,1024]{1,2,0:T(8,128)}, u32[]{:S(2)}, u32[]{:S(2)}) async-start(f32[4,128,1024]{1,2,0:T(8,128)} %get-tuple-element.19), calls=%async_computation.3 | async-start | bytes 4194304 | tf_op jit(solution)/shard_map/all_to_all | solution.py:113
  185.4 2.7 copy-start.6
  188.2 2.0 copy-start.10
  311.6 2.1 copy-start.4
  326.0 2.1 slice-start
  328.1 2.2 copy-start.12
  328.1 2.4 copy-start.8
  328.1 2.4 copy-start.9
  328.1 3.8 %copy-start.1 = (f32[256,1024]{1,0:T(8,128)S(1)}, f32[256,1024]{1,0:T(8,128)}, u32[]{:S(2)}) copy-start(f32[256,1024]{1,0:T(8,128)} %param.7) | copy-start | bytes 3145732
  330.2 1.6 copy-start.11
where the time goes:
time: 333 us; the launch traced here: 332 us
  blocking collectives  176 us (53%)
  local copies, waits for them, and re-layouts  85.9 us (26%)
  waiting for transfers between devices  29.2 us (9%)
  other arithmetic  22.3 us (7%)
  starting transfers between devices  16.5 us (5%)
    all_to_all x2, blocking collectives, in_one_piece(): lax.all_to_all(both, axis, split_axis=split_dim, concat_axis=concat_dim,...  176 us
    gather x20, local copies, waits for them, and re-layouts, pack_rows(): member[source]  27.1 us
    all_to_all x1, waiting for transfers between devices, on_device(): lax.all_to_all(policy, 'gy', split_axis=0, concat_axis=0, tiled=True)  17.8 us
    gather x12, local copies, waits for them, and re-layouts, settle(): return tuple((member[source] for member in payload))  17.5 us
    split x12, local copies, waits for them, and re-layouts, in_one_piece(): jnp.split(lax.all_to_all(both, axis, split_axis=split_dim, concat_axis=co...  12.7 us
    select_n x9, other arithmetic, pack_rows(): jnp.where(filled[:, None], member[source], jnp.float32(empty_value))  11.3 us
    all_to_all x1, waiting for transfers between devices, on_device(): lax.all_to_all(older, 'gy', split_axis=0, concat_axis=0, tiled=True)  10.4 us
    scatter x3, local copies, waits for them, and re-layouts, settle(): source = jnp.zeros((local_rows,), jnp.int32).at[landing].set(jnp.arange(l...  7.31 us
  transfers between devices with their start and end apart: 4, of which 3 were waited for; matrix products, arithmetic and copies ran while one was open for 12% of the time, Pallas kernels for 0%

commit v1 on v0

v1 whole, which is shorter than its diff:
```python
import functools

import jax
import jax.numpy as jnp
from jax import lax
from jax.experimental import pallas as pl
from jax.experimental.pallas import tpu as pltpu
from jax.sharding import PartitionSpec as P

GROUP = 16
BETA = 0.2
LANES = 128
HEAD = 8
MESH = pl.DeviceIdType.MESH
F32 = jnp.float32
BF16 = jnp.bfloat16


def log2(n):
    return n.bit_length() - 1


def iota(shape, dim):
    return lax.broadcasted_iota(jnp.int32, shape, dim)


def dot(a, b):
    return jnp.dot(a, b, preferred_element_type=F32)


def pick(onehot, x, terms):
    total, rest = None, x
    for t in range(terms):
        part = rest.astype(BF16)
        if t < terms - 1:
            rest = rest - part.astype(F32)
        got = dot(onehot, part)
        total = got if total is None else total + got
    return total


def to_column(row):
    n = row.shape[1]
    parts = []
    for t in range(n // LANES):
        tile = row[:, t * LANES : (t + 1) * LANES]
        eye = iota((LANES, LANES), 0) == iota((LANES, LANES), 1)
        parts.append(
            jnp.sum(jnp.where(eye, jnp.broadcast_to(tile, (LANES, LANES)), 0.0), axis=1, keepdims=True)
        )
    return jnp.concatenate(parts, axis=0)


def kernel(
    sizes, chunks, dest_ref, len_ref, mix_ref, lp_ref, rp_ref, rw_ref, tok_ref, adv_ref,
    upper, hot1, hot2, hot3, hot4, lens, wcol,
    rxs, rxr, rys, ryr, rzs, rzr, ws, wr,
    xs, xr, ys, yr, zg, zs, zr,
    rsend, rrecv, xsend, xrecv, ysend, yrecv, zsend, zrecv,
):
    nx, ny, nz = sizes
    rows = lp_ref.shape[0]
    slots = 2 * rows
    cx, cy, cz = slots // nx, slots // ny, slots // nz
    per_tile = LANES // cz
    mx, my, mz = lax.axis_index("gx"), lax.axis_index("gy"), lax.axis_index("gz")
    ring = {"gx": (mx, nx), "gy": (my, ny), "gz": (mz, nz)}

    def peer(axis, step):
        me, n = ring[axis]
        return {axis: lax.rem(me + (step + n), n)}

    barrier = pltpu.get_barrier_semaphore()
    for axis in ("gx", "gy", "gz"):
        for k in range(1, ring[axis][1]):
            pl.semaphore_signal(barrier, inc=1, device_id=peer(axis, k), device_id_type=MESH)

    def send(axis, k, src, dst, ssem, rsem):
        pltpu.make_async_remote_copy(
            src_ref=src, dst_ref=dst, send_sem=ssem, recv_sem=rsem,
            device_id=peer(axis, k), device_id_type=MESH,
        ).start()

    def drain(ref, sem):
        pltpu.make_async_copy(ref, ref, sem).wait()

    upper[...] = jnp.where(iota((slots, slots), 0) < iota((slots, slots), 1), 1.0, 0.0).astype(BF16)

    def slots_of(digit, valid, me, fanout, capacity):
        n = digit.shape[1]
        step = lax.rem(digit - me + fanout, fanout)
        groups = max(fanout, 8)
        member = jnp.where((iota((groups, n), 0) == step) & valid, 1.0, 0.0)
        before = dot(member.astype(BF16), upper[0:n, 0:n])
        rank = jnp.sum(member * before, axis=0, keepdims=True).astype(jnp.int32)
        return jnp.where(valid, step * capacity + rank, -1)

    def one_hot(slot, count):
        n = slot.shape[1]
        return jnp.where(iota((count, n), 0) == slot, 1.0, 0.0).astype(BF16)

    def carry(head, hot):
        return lax.dot_general(
            head.astype(BF16), hot, (((1,), (1,)), ((), ())), preferred_element_type=F32
        )

    dest = jnp.concatenate([dest_ref[t : t + 1, :] for t in range(rows // LANES)], axis=1)
    tx = dest >> log2(rows * ny * nz)
    ty = (dest >> log2(rows * nz)) & (ny - 1)
    tz = (dest >> log2(rows)) & (nz - 1)
    local = dest & (rows - 1)
    field = iota((HEAD, rows), 0)
    head = jnp.where(
        field == 0, ty, jnp.where(field == 1, tz, jnp.where(field == 2, local, jnp.where(field == 3, 1, 0)))
    ).astype(F32)
    hot1[...] = one_hot(slots_of(tx, dest >= 0, mx, nx, cx), slots)
    head = carry(head, hot1[...])
    got = pick(hot1[...], rw_ref[...], 3)
    for k in range(nx):
        to = rxr if k == 0 else rxs
        to[k, 0:HEAD, :] = head[:, k * cx : (k + 1) * cx]
        to[k, HEAD:, :] = got[k * cx : (k + 1) * cx, :]
    pl.semaphore_wait(barrier, (nx - 1) + (ny - 1) + (nz - 1))
    for k in range(1, nx):
        send("gx", k, rxs.at[k], rxr.at[k], rsend.at[0], rrecv.at[0])

    len_row = jnp.concatenate([len_ref[t : t + 1, :] for t in range(rows // LANES)], axis=1)
    lens[...] = jnp.broadcast_to(to_column(len_row.astype(F32)), (rows, LANES)).astype(jnp.int32)

    @pl.loop(0, chunks)
    def _(c):
        columns = pl.ds(pl.multiple_of(c * LANES, LANES), LANES)
        inside = (iota((rows, LANES), 1) + c * LANES) < lens[...]
        policy = lp_ref[:, columns]
        gap = rp_ref[:, columns] - policy
        penalty = jnp.exp(gap) - gap - 1.0
        both = jnp.concatenate(
            [jnp.where(inside, policy, 0.0), jnp.where(inside, BETA * penalty, 0.0)], axis=1
        )
        got = pick(hot1[...], both, 2)
        xr[c, 0:cx, :] = got[0:cx, :]
        xs[c] = got
        for k in range(1, nx):
            at = pl.ds(k * cx, cx)
            send("gx", k, xs.at[c, at], xr.at[c, at], xsend.at[c], xrecv.at[c])

    drain(rxr.at[pl.ds(1, nx - 1)], rrecv.at[0])
    head = jnp.concatenate([rxr[k, 0:HEAD, :] for k in range(nx)], axis=1)
    held = head.astype(jnp.int32)
    hot2[...] = one_hot(slots_of(held[0:1, :], held[3:4, :] > 0, my, ny, cy), slots)
    head = carry(head, hot2[...])
    got = pick(hot2[...], rxr[:, HEAD:, :].reshape(slots, LANES), 3)
    for k in range(ny):
        to = ryr if k == 0 else rys
        to[k, 0:HEAD, :] = head[:, k * cy : (k + 1) * cy]
        to[k, HEAD:, :] = got[k * cy : (k + 1) * cy, :]
    for k in range(1, ny):
        send("gy", k, rys.at[k], ryr.at[k], rsend.at[1], rrecv.at[1])

    def to_y(c):
        drain(xr.at[c, pl.ds(cx, slots - cx)], xrecv.at[c])
        got = pick(hot2[...], xr[c], 2)
        yr[c, 0:cy, :] = got[0:cy, :]
        ys[c] = got
        for k in range(1, ny):
            at = pl.ds(k * cy, cy)
            send("gy", k, ys.at[c, at], yr.at[c, at], ysend.at[c], yrecv.at[c])

    drain(ryr.at[pl.ds(1, ny - 1)], rrecv.at[1])
    head = jnp.concatenate([ryr[k, 0:HEAD, :] for k in range(ny)], axis=1)
    held = head.astype(jnp.int32)
    hot3[...] = one_hot(slots_of(held[1:2, :], held[3:4, :] > 0, mz, nz, cz), slots)
    head = carry(head, hot3[...])
    got = pick(hot3[...], ryr[:, HEAD:, :].reshape(slots, LANES), 3)
    for k in range(nz):
        to = rzr if k == 0 else rzs
        tile = k // per_tile * LANES
        to[k, 0:HEAD, :] = head[:, tile : tile + LANES]
        to[k, HEAD:, :] = got[k * cz : (k + 1) * cz, :]
    for k in range(1, nz):
        send("gz", k, rzs.at[k], rzr.at[k], rsend.at[2], rrecv.at[2])

    def along_slots(tiles):
        spot = iota((HEAD, LANES), 1) // cz
        parts = []
        for t in range(nz // per_tile):
            part = tiles(t * per_tile)
            for j in range(1, per_tile):
                part = jnp.where(spot == j, tiles(t * per_tile + j), part)
            parts.append(part)
        return jnp.concatenate(parts, axis=1)

    to_y(0)
    to_y(1)

    drain(rzr.at[pl.ds(1, nz - 1)], rrecv.at[2])
    held = along_slots(lambda k: rzr[k, 0:HEAD, :]).astype(jnp.int32)
    place = jnp.where(held[3:4, :] > 0, held[2:3, :], -1)
    chosen = iota((rows, slots), 0) == place
    hot4[...] = jnp.where(chosen, 1.0, 0.0).astype(BF16)
    judged = pick(hot4[...], rzr[:, HEAD:, :].reshape(slots, LANES), 3)
    grouped = judged.reshape(rows // GROUP, GROUP, LANES)
    centre = jnp.mean(grouped, axis=1, keepdims=True)
    deviation = grouped - centre
    spread = jnp.mean(deviation * deviation, axis=1, keepdims=True)
    advantages = (deviation / jnp.sqrt(spread + 1.0)).reshape(rows, LANES)
    adv_ref[...] = advantages
    weight = jnp.sum(advantages * mix_ref[...], axis=1, keepdims=True)
    row = jnp.sum(jnp.where(chosen, weight, 0.0), axis=0, keepdims=True)
    for t in range(nz // per_tile):
        ws[t] = jnp.broadcast_to(row[:, t * LANES : (t + 1) * LANES], (HEAD, LANES))
    wr[0] = jnp.broadcast_to(row[:, 0:LANES], (HEAD, LANES))
    for k in range(1, nz):
        send("gz", -k, ws.at[k // per_tile], wr.at[k], rsend.at[3], rrecv.at[3])

    def gather_z(c):
        drain(yr.at[c, pl.ds(cy, slots - cy)], yrecv.at[c])
        zg[c] = pick(hot3[...], yr[c], 2)

    def send_z(c):
        loss = zg[c, :, LANES:] - wcol[...] * zg[c, :, 0:LANES]
        zr[c, 0:cz, :] = loss[0:cz, :]
        zs[c] = loss
        for k in range(1, nz):
            at = pl.ds(k * cz, cz)
            send("gz", k, zs.at[c, at], zr.at[c, at], zsend.at[c], zrecv.at[c])

    gather_z(0)
    drain(wr.at[pl.ds(1, nz - 1)], rrecv.at[3])
    wcol[...] = jnp.broadcast_to(to_column(along_slots(lambda k: wr[k])[0:1, :]), (slots, LANES))
    send_z(0)

    @pl.loop(2, chunks)
    def _(c):
        to_y(c)
        gather_z(c - 1)
        send_z(c - 1)

    gather_z(chunks - 1)
    send_z(chunks - 1)

    @pl.loop(0, chunks)
    def _(c):
        drain(zr.at[c, pl.ds(cz, slots - cz)], zrecv.at[c])
        columns = pl.ds(pl.multiple_of(c * LANES, LANES), LANES)
        tok_ref[:, columns] = pick(hot4[...], zr[c], 2)

    drain(rxs.at[pl.ds(1, nx - 1)], rsend.at[0])
    drain(rys.at[pl.ds(1, ny - 1)], rsend.at[1])
    drain(rzs.at[pl.ds(1, nz - 1)], rsend.at[2])
    drain(wr.at[pl.ds(1, nz - 1)], rsend.at[3])

    @pl.loop(0, chunks)
    def _(c):
        drain(xs.at[c, pl.ds(cx, slots - cx)], xsend.at[c])
        drain(ys.at[c, pl.ds(cy, slots - cy)], ysend.at[c])
        drain(zs.at[c, pl.ds(cz, slots - cz)], zsend.at[c])


def on_device(sizes, log_probs, ref_log_probs, rewards, destination, lengths, mixing):
    rows, width = log_probs.shape
    slots = 2 * rows
    chunks = width // LANES
    nx, ny, nz = sizes
    vmem = pl.BlockSpec(memory_space=pltpu.VMEM)
    wide = pltpu.VMEM((chunks, slots, 2 * LANES), F32)
    thin = pltpu.VMEM((chunks, slots, LANES), F32)
    sem = pltpu.SemaphoreType.DMA

    def reward_buffer(n):
        return pltpu.VMEM((n, HEAD + slots // n, LANES), F32)

    return pl.pallas_call(
        functools.partial(kernel, sizes, chunks),
        out_shape=(
            jax.ShapeDtypeStruct((rows, width), F32),
            jax.ShapeDtypeStruct((rows, LANES), F32),
        ),
        in_specs=[vmem] * 6,
        out_specs=(vmem, vmem),
        scratch_shapes=[
            pltpu.VMEM((slots, slots), BF16),
            pltpu.VMEM((slots, rows), BF16),
            pltpu.VMEM((slots, slots), BF16),
            pltpu.VMEM((slots, slots), BF16),
            pltpu.VMEM((rows, slots), BF16),
            pltpu.VMEM((rows, LANES), jnp.int32),
            pltpu.VMEM((slots, LANES), F32),
            reward_buffer(nx), reward_buffer(nx),
            reward_buffer(ny), reward_buffer(ny),
            reward_buffer(nz), reward_buffer(nz),
            pltpu.VMEM((slots // LANES, HEAD, LANES), F32),
            pltpu.VMEM((nz, HEAD, LANES), F32),
            wide, wide, wide, wide, wide, thin, thin,
            sem((4,)), sem((4,)),
            sem((chunks,)), sem((chunks,)), sem((chunks,)), sem((chunks,)), sem((chunks,)), sem((chunks,)),
        ],
        compiler_params=pltpu.CompilerParams(
            collective_id=0, has_side_effects=True, vmem_limit_bytes=60 << 20
        ),
        name="regroup",
    )(
        destination.reshape(rows // LANES, LANES),
        lengths.reshape(rows // LANES, LANES),
        mixing.reshape(1, LANES),
        log_probs,
        ref_log_probs,
        rewards,
    )


def solution(mesh):
    sizes = tuple(mesh.shape[a] for a in ("gx", "gy", "gz"))
    rows = P(("gx", "gy", "gz"), None)
    flat = P(("gx", "gy", "gz"))
    return jax.shard_map(
        functools.partial(on_device, sizes),
        mesh=mesh,
        in_specs=(rows, rows, rows, flat, flat, P()),
        out_specs=(rows, rows),
        check_vma=False,
    )
```

time: 333 us -> 92.6 us (0.28)
  blocking collectives: 176 us -> 0 us
  Pallas kernels: 0 us -> 88.8 us
  local copies, waits for them, and re-layouts: 85.9 us -> 3 us
  waiting for transfers between devices: 29.2 us -> 0 us
  other arithmetic: 22.3 us -> 0 us
  starting transfers between devices: 16.5 us -> 0 us
    all_to_all x2 -> x0, blocking collectives: 176 us -> none  [in_one_piece(): lax.all_to_all(both, axis, split_axis=split_dim, concat_axis=concat_dim,...]
    pallas_call x0 -> x1, Pallas kernels: none -> 88.8 us  [on_device(): pl.pallas_call(functools.partial(kernel, sizes, chunks), out_shape=(jax.S...]
    gather x32 -> x0, local copies, waits for them, and re-layouts: 44.6 us -> none  [the longest x20 27.1 us: pack_rows(): member[source]]
    all_to_all x4 -> x0, waiting for transfers between devices: 29.2 us -> none  [the longest x1 17.8 us: on_device(): lax.all_to_all(policy, 'gy', split_axis=0, concat_axis=0, tiled=True)]
    all_to_all x4 -> x0, starting transfers between devices: 16.5 us -> none  [the longest x1 4.44 us: on_device(): lax.all_to_all(older, 'gy', split_axis=0, concat_axis=0, tiled=True)]
    scatter x9 -> x0, local copies, waits for them, and re-layouts: 15.9 us -> none  [the longest x3 7.31 us: settle(): source = jnp.zeros((local_rows,), jnp.int32).at[landing].set(jnp.arange(l...]
    select_n x25 -> x0, other arithmetic: 14.7 us -> none  [the longest x9 11.3 us: pack_rows(): jnp.where(filled[:, None], member[source], jnp.float32(empty_value))]
    split x12 -> x0, local copies, waits for them, and re-layouts: 12.7 us -> none  [in_one_piece(): jnp.split(lax.all_to_all(both, axis, split_axis=split_dim, concat_axis=co...]
  transfers between devices with their start and end apart: 4 -> 0, of which waited for: 3 -> 0; matrix products, arithmetic and copies ran while one was open for 12% -> 0% of each run, Pallas kernels for 0% -> 0%
where the time goes in v1:
time: 92.6 us; the launch traced here: 92.5 us
  Pallas kernels  88.8 us (96%)
  local copies, waits for them, and re-layouts  3 us (3%)
    pallas_call x1, Pallas kernels, on_device(): pl.pallas_call(functools.partial(kernel, sizes, chunks), out_shape=(jax.S...  88.8 us
    unnamed x4, local copies, waits for them, and re-layouts  3 us

profile of v1, /device:TPU:1, one launch (start us, length us, event | category | flops | bytes accessed | tf_op | source)
XLA Modules:
  0.0 92.5 jit_solution(4037102345871820749)
XLA Ops:
  0.6 88.8 %regroup.1 = (f32[256,1024]{1,0:T(8,128)}, f32[256,128]{1,0:T(8,128)}) custom-call(s32[2,128]{1,0:T(2,128)} %bitcast.3, s32[2,128]{1,0:T(2,128)} %bitcast.4, f32[1,128]{1,0:T(1,128)} %bitcast.5, f32[256,1024]{1,0:T(8,128)} %lp_ref.1, f32[256,1024]{1,0:T(8,128)} %rp_ref.1, f32[256,128]{1,0:T(8,128)} %rw_ref.1), custom_call_target="tpu_custom_call" | custom-call | tf_op jit(solution)/shard_map/regroup/pallas_call | solution.py:273
  89.5 0.0 copy-start
  89.5 2.3 %copy.10 = f32[256,1024]{1,0:T(8,128)} copy(f32[256,1024]{1,0:T(8,128)} %get-tuple-element.4) | data formatting | bytes 2097152
  91.8 0.0 copy-done
  91.8 0.7 copy.11
Async XLA Ops:
  89.5 2.4 %copy-start = (f32[256,128]{1,0:T(8,128)S(1)}, f32[256,128]{1,0:T(8,128)}, u32[]{:S(2)}) copy-start(f32[256,128]{1,0:T(8,128)} %get-tuple-element.5) | copy-start | bytes 393220

commit v2 on v1

v2 whole, which is shorter than its diff:
```python
import functools

import jax
import jax.numpy as jnp
from jax import lax
from jax.experimental import pallas as pl
from jax.experimental.pallas import tpu as pltpu
from jax.sharding import PartitionSpec as P

GROUP = 16
BETA = 0.2
LANES = 128
HALF = LANES // 2
HEAD = 8
MESH = pl.DeviceIdType.MESH
F32 = jnp.float32
BF16 = jnp.bfloat16


def log2(n):
    return n.bit_length() - 1


def iota(shape, dim):
    return lax.broadcasted_iota(jnp.int32, shape, dim)


def dot(a, b):
    return jnp.dot(a, b, preferred_element_type=F32)


def pick(onehot, x, terms):
    total, rest = None, x
    for t in range(terms):
        part = rest.astype(BF16)
        if t < terms - 1:
            rest = rest - part.astype(F32)
        got = dot(onehot, part)
        total = got if total is None else total + got
    return total


def low():
    return iota((1, LANES), 1) < HALF


def swap(x):
    return pltpu.roll(x, HALF, 1)


def to_column(row):
    n = row.shape[1]
    parts = []
    for t in range(n // LANES):
        tile = row[:, t * LANES : (t + 1) * LANES]
        eye = iota((LANES, LANES), 0) == iota((LANES, LANES), 1)
        parts.append(
            jnp.sum(jnp.where(eye, jnp.broadcast_to(tile, (LANES, LANES)), 0.0), axis=1, keepdims=True)
        )
    return jnp.concatenate(parts, axis=0)


def kernel(
    sizes, chunks, dest_hbm, len_hbm, mix_hbm, lp_hbm, rp_hbm, rw_hbm, tok_ref, adv_ref,
    dest_ref, len_ref, mix_ref, lp_ref, rp_ref, rw_ref,
    upper, hot1, hot2, hot3, hot4, lens, wcol, wrow,
    hxs, hxr, hys, hyr, hzs, hzr, ws, wr,
    rxs, rxr, rys, ryr, rzs, rzr,
    xs, xr, ys, yr, zg, zs, zr,
    loads, hsend, hrecv, rsend, rrecv, xsend, xrecv, ysend, yrecv, zsend, zrecv,
):
    nx, ny, nz = sizes
    rows = lp_ref.shape[0]
    slots = 2 * rows
    cx, cy, cz = slots // nx, slots // ny, slots // nz
    per_tile = LANES // cz
    tiles = slots // LANES
    mx, my, mz = lax.axis_index("gx"), lax.axis_index("gy"), lax.axis_index("gz")
    ring = {"gx": (mx, nx), "gy": (my, ny), "gz": (mz, nz)}

    def far_first(n):
        return sorted(range(1, n), key=lambda k: -min(k, n - k))

    def peer(axis, step):
        me, n = ring[axis]
        return {axis: lax.rem(me + (step + n), n)}

    fetches = [
        pltpu.make_async_copy(a, b, loads.at[i])
        for i, (a, b) in enumerate(
            (
                (dest_hbm, dest_ref), (rw_hbm, rw_ref), (len_hbm, len_ref),
                (lp_hbm, lp_ref), (rp_hbm, rp_ref), (mix_hbm, mix_ref),
            )
        )
    ]
    for fetch in fetches:
        fetch.start()

    barrier = pltpu.get_barrier_semaphore()
    for axis in ("gz", "gx", "gy"):
        for k in range(1, ring[axis][1]):
            pl.semaphore_signal(barrier, inc=1, device_id=peer(axis, k), device_id_type=MESH)

    def send(axis, k, src, dst, ssem, rsem):
        pltpu.make_async_remote_copy(
            src_ref=src, dst_ref=dst, send_sem=ssem, recv_sem=rsem,
            device_id=peer(axis, k), device_id_type=MESH,
        ).start()

    def drain(ref, sem):
        pltpu.make_async_copy(ref, ref, sem).wait()

    upper[...] = jnp.where(iota((slots, slots), 0) < iota((slots, slots), 1), 1.0, 0.0).astype(BF16)

    def slots_of(digit, valid, me, fanout, capacity):
        n = digit.shape[1]
        step = lax.rem(digit - me + fanout, fanout)
        groups = max(fanout, 8)
        member = jnp.where((iota((groups, n), 0) == step) & valid, 1.0, 0.0)
        before = dot(member.astype(BF16), upper[0:n, 0:n])
        rank = jnp.sum(member * before, axis=0, keepdims=True).astype(jnp.int32)
        return jnp.where(valid, step * capacity + rank, -1)

    def one_hot(slot, count):
        n = slot.shape[1]
        return jnp.where(iota((count, n), 0) == slot, 1.0, 0.0).astype(BF16)

    def carry(head, hot):
        return lax.dot_general(
            head.astype(BF16), hot, (((1,), (1,)), ((), ())), preferred_element_type=F32
        )

    def spread_rewards(hot, x, n, own, out):
        got = pick(hot, x, 3)
        c = slots // n // 2
        first = got.reshape(n, 2, c, LANES)[:, 0]
        last = swap(got).reshape(n, 2, c, LANES)[:, 1]
        packed = jnp.where(low()[None], first, last)
        own[0] = packed[0]
        out[...] = packed

    def unpacked(ref):
        n, c = ref.shape[0], ref.shape[1]
        x = ref[...]
        y = swap(x.reshape(n * c, LANES)).reshape(n, c, LANES)
        return jnp.concatenate([x, y], axis=1).reshape(slots, LANES)

    def along_slots(tile):
        spot = iota((HEAD, LANES), 1) // cz
        parts = []
        for t in range(tiles):
            part = tile(t * per_tile)
            for j in range(1, per_tile):
                part = jnp.where(spot == j, tile(t * per_tile + j), part)
            parts.append(part)
        return jnp.concatenate(parts, axis=1)

    fetches[0].wait()
    dest = jnp.concatenate([dest_ref[t : t + 1, :] for t in range(rows // LANES)], axis=1)
    tx = dest >> log2(rows * ny * nz)
    ty = (dest >> log2(rows * nz)) & (ny - 1)
    tz = (dest >> log2(rows)) & (nz - 1)
    local = dest & (rows - 1)
    field = iota((HEAD, rows), 0)
    head = jnp.where(
        field == 0, ty, jnp.where(field == 1, tz, jnp.where(field == 2, local, jnp.where(field == 3, 1, 0)))
    ).astype(F32)
    hot1[...] = one_hot(slots_of(tx, dest >= 0, mx, nx, cx), slots)
    head = carry(head, hot1[...])
    hxr[0] = head[:, 0:cx]
    for k in range(1, nx):
        hxs[k] = head[:, k * cx : (k + 1) * cx]
    fetches[1].wait()
    spread_rewards(hot1[...], rw_ref[...], nx, rxr.at[0], rxs.at[0])
    def send_rewards(axis, hop, half, out, into):
        for k in far_first(ring[axis][1]):
            at = 2 * hop + half
            send(axis, k, out.at[half, k], into.at[half, k], rsend.at[at], rrecv.at[at])

    def drain_rewards(hop, half, ref, sem):
        drain(ref.at[half, pl.ds(1, ref.shape[1] - 1)], sem.at[2 * hop + half])

    pl.semaphore_wait(barrier, (nx - 1) + (ny - 1) + (nz - 1))
    send_rewards("gx", 0, 0, rxs, rxr)
    for k in far_first(nx):
        send("gx", k, hxs.at[k], hxr.at[k], hsend.at[0], hrecv.at[0])
    spread_rewards(hot1[...], swap(rw_ref[...]), nx, rxr.at[1], rxs.at[1])
    send_rewards("gx", 0, 1, rxs, rxr)
    fetches[2].wait()
    len_row = jnp.concatenate([len_ref[t : t + 1, :] for t in range(rows // LANES)], axis=1)
    lens[...] = jnp.broadcast_to(to_column(len_row.astype(F32)), (rows, LANES)).astype(jnp.int32)
    fetches[3].wait()
    fetches[4].wait()

    def to_x(c):
        columns = pl.ds(pl.multiple_of(c * LANES, LANES), LANES)
        inside = (iota((rows, LANES), 1) + c * LANES) < lens[...]
        policy = lp_ref[:, columns]
        gap = rp_ref[:, columns] - policy
        penalty = jnp.exp(gap) - gap - 1.0
        policy = jnp.where(inside, policy, 0.0)
        penalty = jnp.where(inside, BETA * penalty, 0.0)
        other = swap(policy)
        both = jnp.concatenate(
            [jnp.where(low(), penalty, other), jnp.where(low(), other, penalty)], axis=1
        )
        got = pick(hot1[...], both, 2)
        for h in range(2):
            part = got[:, h * LANES : (h + 1) * LANES]
            xr[2 * c + h, 0:cx, :] = part[0:cx, :]
            xs[2 * c + h] = part
            for k in far_first(nx):
                at = pl.ds(k * cx, cx)
                send(
                    "gx", k, xs.at[2 * c + h, at], xr.at[2 * c + h, at],
                    xsend.at[2 * c + h], xrecv.at[2 * c + h],
                )

    def to_y(c):
        drain(xr.at[c, pl.ds(cx, slots - cx)], xrecv.at[c])
        got = pick(hot2[...], xr[c], 2)
        yr[c, 0:cy, :] = got[0:cy, :]
        ys[c] = got
        for k in far_first(ny):
            at = pl.ds(k * cy, cy)
            send("gy", k, ys.at[c, at], yr.at[c, at], ysend.at[c], yrecv.at[c])

    def drain_y(c):
        drain(yr.at[c, pl.ds(cy, slots - cy)], yrecv.at[c])

    def gather_z(c):
        drain_y(2 * c)
        drain_y(2 * c + 1)
        return pick(hot3[...], jnp.concatenate([yr[2 * c], yr[2 * c + 1]], axis=1), 2)

    def loss(even, odd, weights):
        return jnp.where(low(), even, odd) - weights * swap(jnp.where(low(), odd, even))

    def send_z(c, rows_out):
        zr[c, 0:cz, :] = rows_out[0:cz, :]
        zs[c] = rows_out
        for k in far_first(nz):
            at = pl.ds(k * cz, cz)
            send("gz", k, zs.at[c, at], zr.at[c, at], zsend.at[c], zrecv.at[c])

    to_x(0)

    drain(hxr.at[pl.ds(1, nx - 1)], hrecv.at[0])
    head = jnp.concatenate([hxr[k] for k in range(nx)], axis=1)
    held = head.astype(jnp.int32)
    hot2[...] = one_hot(slots_of(held[0:1, :], held[3:4, :] > 0, my, ny, cy), slots)
    head = carry(head, hot2[...])
    hyr[0] = head[:, 0:cy]
    for k in range(1, ny):
        hys[k] = head[:, k * cy : (k + 1) * cy]
    for k in far_first(ny):
        send("gy", k, hys.at[k], hyr.at[k], hsend.at[1], hrecv.at[1])

    for half in range(2):
        drain_rewards(0, half, rxr, rrecv)
        spread_rewards(hot2[...], unpacked(rxr.at[half]), ny, ryr.at[half], rys.at[half])
        send_rewards("gy", 1, half, rys, ryr)

    to_x(1)

    drain(hyr.at[pl.ds(1, ny - 1)], hrecv.at[1])
    head = jnp.concatenate([hyr[k] for k in range(ny)], axis=1)
    held = head.astype(jnp.int32)
    hot3[...] = one_hot(slots_of(held[1:2, :], held[3:4, :] > 0, mz, nz, cz), slots)
    head = carry(head, hot3[...])
    hzr[0] = head[:, 0:LANES]
    for t in range(tiles):
        hzs[t] = head[:, t * LANES : (t + 1) * LANES]
    for k in far_first(nz):
        send("gz", k, hzs.at[k // per_tile], hzr.at[k], hsend.at[2], hrecv.at[2])

    def rewards_to_z(half):
        drain_rewards(1, half, ryr, rrecv)
        spread_rewards(hot3[...], unpacked(ryr.at[half]), nz, rzr.at[half], rzs.at[half])
        send_rewards("gz", 2, half, rzs, rzr)

    rewards_to_z(0)
    to_y(0)
    rewards_to_z(1)
    to_x(2)
    drain(hzr.at[pl.ds(1, nz - 1)], hrecv.at[2])
    held = along_slots(lambda k: hzr[k]).astype(jnp.int32)
    place = jnp.where(held[3:4, :] > 0, held[2:3, :], -1)
    hot4[...] = jnp.where(iota((rows, slots), 0) == place, 1.0, 0.0).astype(BF16)
    to_y(1)
    to_x(3)
    fetches[5].wait()

    drain_y(0)
    send_z(0, pick(hot3[...], yr[0], 2))
    to_y(2)
    to_x(4)
    to_y(3)
    drain_y(1)
    zg[...] = pick(hot3[...], yr[1], 2)

    drain_rewards(2, 0, rzr, rrecv)
    judged = pick(hot4[...], unpacked(rzr.at[0]), 3)
    drain_rewards(2, 1, rzr, rrecv)
    judged = jnp.where(low(), judged, swap(pick(hot4[...], unpacked(rzr.at[1]), 3)))
    grouped = judged.reshape(rows // GROUP, GROUP, LANES)
    centre = jnp.mean(grouped, axis=1, keepdims=True)
    deviation = grouped - centre
    spread = jnp.mean(deviation * deviation, axis=1, keepdims=True)
    advantages = (deviation / jnp.sqrt(spread + 1.0)).reshape(rows, LANES)
    weight = jnp.sum(advantages * mix_ref[...], axis=1, keepdims=True)
    row = jnp.sum(hot4[...].astype(F32) * weight, axis=0, keepdims=True)
    wr[0] = jnp.broadcast_to(row[:, 0:LANES], (HEAD, LANES))
    for t in range(tiles):
        ws[t] = jnp.broadcast_to(row[:, t * LANES : (t + 1) * LANES], (HEAD, LANES))
    for k in far_first(nz):
        send("gz", -k, ws.at[k // per_tile], wr.at[k], rsend.at[6], rrecv.at[6])
    send_z(chunks, zg[...])
    adv_ref[...] = advantages
    wrow[...] = jnp.broadcast_to(weight, (rows, LANES))

    to_y(4)
    to_x(5)
    to_y(5)
    second = gather_z(1)
    to_y(6)
    drain(wr.at[pl.ds(1, nz - 1)], rrecv.at[6])
    wcol[...] = jnp.broadcast_to(to_column(along_slots(lambda k: wr[k])[0:1, :]), (slots, LANES))
    send_z(1, loss(second[:, 0:LANES], second[:, LANES:], wcol[...]))
    to_x(6)
    to_y(7)
    to_x(7)

    def loss_to_z(c):
        got = gather_z(c)
        send_z(c, loss(got[:, 0:LANES], got[:, LANES:], wcol[...]))

    @pl.loop(2, chunks - 2)
    def _(c):
        loss_to_z(c)
        to_y(2 * c + 4)
        to_y(2 * c + 5)

    @pl.loop(chunks - 2, chunks)
    def _(c):
        loss_to_z(c)

    for i, (h, r, n) in enumerate(((hxr, rxr, nx), (hyr, ryr, ny), (hzr, rzr, nz))):
        drain(h.at[pl.ds(1, n - 1)], hsend.at[i])
        drain_rewards(i, 0, r, rsend)
        drain_rewards(i, 1, r, rsend)
    drain(wr.at[pl.ds(1, nz - 1)], rsend.at[6])

    @pl.loop(0, 2 * chunks)
    def _(c):
        drain(xs.at[c, pl.ds(cx, slots - cx)], xsend.at[c])
        drain(ys.at[c, pl.ds(cy, slots - cy)], ysend.at[c])

    def arrived(c):
        drain(zr.at[c, pl.ds(cz, slots - cz)], zrecv.at[c])
        return pick(hot4[...], zr[c], 2)

    even = arrived(0)
    tok_ref[:, 0:LANES] = loss(even, arrived(chunks), wrow[...])

    @pl.loop(1, chunks)
    def _(c):
        columns = pl.ds(pl.multiple_of(c * LANES, LANES), LANES)
        tok_ref[:, columns] = arrived(c)

    @pl.loop(0, chunks + 1)
    def _(c):
        drain(zs.at[c, pl.ds(cz, slots - cz)], zsend.at[c])


def on_device(sizes, log_probs, ref_log_probs, rewards, destination, lengths, mixing):
    rows, width = log_probs.shape
    slots = 2 * rows
    chunks = width // LANES
    nx, ny, nz = sizes
    wide = pltpu.VMEM((2 * chunks, slots, LANES), F32)
    thin = pltpu.VMEM((chunks + 1, slots, LANES), F32)
    sem = pltpu.SemaphoreType.DMA

    def head_buffer(n):
        return pltpu.VMEM((n, HEAD, LANES), F32)

    def reward_buffer(n):
        return pltpu.VMEM((2, n, slots // n // 2, LANES), F32)

    return pl.pallas_call(
        functools.partial(kernel, sizes, chunks),
        out_shape=(pltpu.VMEM((rows, width), F32), pltpu.VMEM((rows, LANES), F32)),
        in_specs=[pl.BlockSpec(memory_space=pl.ANY)] * 6,
        out_specs=(pl.BlockSpec(memory_space=pltpu.VMEM),) * 2,
        scratch_shapes=[
            pltpu.VMEM((rows // LANES, LANES), jnp.int32),
            pltpu.VMEM((rows // LANES, LANES), jnp.int32),
            pltpu.VMEM((1, LANES), F32),
            pltpu.VMEM((rows, width), F32),
            pltpu.VMEM((rows, width), F32),
            pltpu.VMEM((rows, LANES), F32),
            pltpu.VMEM((slots, slots), BF16),
            pltpu.VMEM((slots, rows), BF16),
            pltpu.VMEM((slots, slots), BF16),
            pltpu.VMEM((slots, slots), BF16),
            pltpu.VMEM((rows, slots), BF16),
            pltpu.VMEM((rows, LANES), jnp.int32),
            pltpu.VMEM((slots, LANES), F32),
            pltpu.VMEM((rows, LANES), F32),
            head_buffer(nx), head_buffer(nx),
            head_buffer(ny), head_buffer(ny),
            head_buffer(slots // LANES), head_buffer(nz),
            head_buffer(slots // LANES), head_buffer(nz),
            reward_buffer(nx), reward_buffer(nx),
            reward_buffer(ny), reward_buffer(ny),
            reward_buffer(nz), reward_buffer(nz),
            wide, wide, wide, wide, pltpu.VMEM((slots, LANES), F32), thin, thin,
            sem((6,)), sem((3,)), sem((3,)), sem((7,)), sem((7,)),
            sem((2 * chunks,)), sem((2 * chunks,)), sem((2 * chunks,)), sem((2 * chunks,)), sem((chunks + 1,)), sem((chunks + 1,)),
        ],
        compiler_params=pltpu.CompilerParams(
            collective_id=0, has_side_effects=True, vmem_limit_bytes=60 << 20
        ),
        name="regroup",
    )(
        destination.reshape(rows // LANES, LANES),
        lengths.reshape(rows // LANES, LANES),
        mixing.reshape(1, LANES),
        log_probs,
        ref_log_probs,
        rewards,
    )


def solution(mesh):
    sizes = tuple(mesh.shape[a] for a in ("gx", "gy", "gz"))
    rows = P(("gx", "gy", "gz"), None)
    flat = P(("gx", "gy", "gz"))
    return jax.shard_map(
        functools.partial(on_device, sizes),
        mesh=mesh,
        in_specs=(rows, rows, rows, flat, flat, P()),
        out_specs=(rows, rows),
        check_vma=False,
    )
```

time: 92.6 us -> 85.3 us (0.921)
  Pallas kernels: 88.8 us -> 82.9 us
  local copies, waits for them, and re-layouts: 3 us -> 1.63 us
    pallas_call x1, Pallas kernels: 88.8 us -> 82.9 us  [on_device(): pl.pallas_call(functools.partial(kernel, sizes, chunks), out_shape=(pltpu...]
    unnamed x4 -> x2, local copies, waits for them, and re-layouts: 3 us -> 1.63 us
where the time goes in v2:
time: 85.3 us; the launch traced here: 85.2 us
  Pallas kernels  82.9 us (97%)
  local copies, waits for them, and re-layouts  1.63 us (2%)
    pallas_call x1, Pallas kernels, on_device(): pl.pallas_call(functools.partial(kernel, sizes, chunks), out_shape=(pltpu...  82.9 us

profile of v2, /device:TPU:1, one launch (start us, length us, event | category | flops | bytes accessed | tf_op | source)
XLA Modules:
  0.0 85.2 jit_solution(13560669020364802563)
XLA Ops:
  0.6 82.9 %regroup.1 = (f32[256,1024]{1,0:T(8,128)S(1)}, f32[256,128]{1,0:T(8,128)S(1)}) custom-call(s32[2,128]{1,0:T(2,128)} %bitcast.3, s32[2,128]{1,0:T(2,128)} %bitcast.4, f32[1,128]{1,0:T(1,128)} %bitcast.5, f32[256,1024]{1,0:T(8,128)} %lp_hbm.1, f32[256,1024]{1,0:T(8,128)} %rp_hbm.1, f32[256,128]{1,0:T(8,128)} %rw_hbm.1), custom_call_target="tpu_custom_call" | custom-call | tf_op jit(solution)/shard_map/regroup/pallas_call | solution.py:392
  83.5 1.0 %copy.10 = f32[256,1024]{1,0:T(8,128)} copy(f32[256,1024]{1,0:T(8,128)S(1)} %get-tuple-element.2) | data formatting | bytes 2097152
  84.5 0.7 copy.11

commit v3 on v2

--- a/solution.py
+++ b/solution.py
@@ -29,15 +29,12 @@
     return jnp.dot(a, b, preferred_element_type=F32)
 
 
-def pick(onehot, x, terms):
-    total, rest = None, x
-    for t in range(terms):
-        part = rest.astype(BF16)
-        if t < terms - 1:
-            rest = rest - part.astype(F32)
-        got = dot(onehot, part)
-        total = got if total is None else total + got
-    return total
+def pick(onehot, x):
+    n = x.shape[1]
+    first = x.astype(BF16)
+    second = (x - first.astype(F32)).astype(BF16)
+    got = dot(onehot, jnp.concatenate([first, second], axis=1))
+    return got[:, 0:n] + got[:, n:]
 
 
 def low():
@@ -46,6 +43,16 @@
 
 def swap(x):
     return pltpu.roll(x, HALF, 1)
+
+
+def pick_half(onehot, x):
+    first = x.astype(BF16).astype(F32)
+    rest = x - first
+    second = rest.astype(BF16).astype(F32)
+    third = (rest - second).astype(BF16)
+    both = jnp.where(low(), first, swap(second)).astype(BF16)
+    got = dot(onehot, jnp.concatenate([both, third], axis=1))
+    return (got[:, 0:LANES] + swap(got[:, 0:LANES])) + got[:, LANES:]
 
 
 def to_column(row):
@@ -66,7 +73,7 @@
     upper, hot1, hot2, hot3, hot4, lens, wcol, wrow,
     hxs, hxr, hys, hyr, hzs, hzr, ws, wr,
     rxs, rxr, rys, ryr, rzs, rzr,
-    xs, xr, ys, yr, zg, zs, zr,
+    xs, xr, ys, yr, zs, zr,
     loads, hsend, hrecv, rsend, rrecv, xsend, xrecv, ysend, yrecv, zsend, zrecv,
 ):
     nx, ny, nz = sizes
@@ -127,12 +134,17 @@
         return jnp.where(iota((count, n), 0) == slot, 1.0, 0.0).astype(BF16)
 
     def carry(head, hot):
-        return lax.dot_general(
-            head.astype(BF16), hot, (((1,), (1,)), ((), ())), preferred_element_type=F32
+        place = head - 1
+        field = iota((HEAD, head.shape[1]), 0)
+        parts = jnp.where(
+            field == 0, place >> 8, jnp.where(field == 1, place & 255, jnp.where(field == 2, 1, 0))
         )
+        parts = jnp.where(head > 0, parts, 0).astype(F32).astype(BF16)
+        got = lax.dot_general(parts, hot, (((1,), (1,)), ((), ())), preferred_element_type=F32)
+        return got[0:1, :] * 256.0 + got[1:2, :] + got[2:3, :]
 
     def spread_rewards(hot, x, n, own, out):
-        got = pick(hot, x, 3)
+        got = pick_half(hot, x)
         c = slots // n // 2
         first = got.reshape(n, 2, c, LANES)[:, 0]
         last = swap(got).reshape(n, 2, c, LANES)[:, 1]
@@ -147,7 +159,7 @@
         return jnp.concatenate([x, y], axis=1).reshape(slots, LANES)
 
     def along_slots(tile):
-        spot = iota((HEAD, LANES), 1) // cz
+        spot = iota((1, LANES), 1) // cz
         parts = []
         for t in range(tiles):
             part = tile(t * per_tile)
@@ -159,33 +171,26 @@
     fetches[0].wait()
     dest = jnp.concatenate([dest_ref[t : t + 1, :] for t in range(rows // LANES)], axis=1)
     tx = dest >> log2(rows * ny * nz)
-    ty = (dest >> log2(rows * nz)) & (ny - 1)
-    tz = (dest >> log2(rows)) & (nz - 1)
-    local = dest & (rows - 1)
-    field = iota((HEAD, rows), 0)
-    head = jnp.where(
-        field == 0, ty, jnp.where(field == 1, tz, jnp.where(field == 2, local, jnp.where(field == 3, 1, 0)))
-    ).astype(F32)
     hot1[...] = one_hot(slots_of(tx, dest >= 0, mx, nx, cx), slots)
-    head = carry(head, hot1[...])
+    head = carry((dest & (rows * ny * nz - 1)) + 1, hot1[...])
     hxr[0] = head[:, 0:cx]
     for k in range(1, nx):
         hxs[k] = head[:, k * cx : (k + 1) * cx]
     fetches[1].wait()
     spread_rewards(hot1[...], rw_ref[...], nx, rxr.at[0], rxs.at[0])
+    spread_rewards(hot1[...], swap(rw_ref[...]), nx, rxr.at[1], rxs.at[1])
     def send_rewards(axis, hop, half, out, into):
         for k in far_first(ring[axis][1]):
             at = 2 * hop + half
-            send(axis, k, out.at[half, k], into.at[half, k], rsend.at[at], rrecv.at[at])
-
-    def drain_rewards(hop, half, ref, sem):
-        drain(ref.at[half, pl.ds(1, ref.shape[1] - 1)], sem.at[2 * hop + half])
+            send(axis, k, out.at[half, k], into.at[half, k], rsend.at[hop], rrecv.at[at])
+
+    def drain_rewards(hop, half, ref):
+        drain(ref.at[half, pl.ds(1, ref.shape[1] - 1)], rrecv.at[2 * hop + half])
 
     pl.semaphore_wait(barrier, (nx - 1) + (ny - 1) + (nz - 1))
-    send_rewards("gx", 0, 0, rxs, rxr)
     for k in far_first(nx):
         send("gx", k, hxs.at[k], hxr.at[k], hsend.at[0], hrecv.at[0])
-    spread_rewards(hot1[...], swap(rw_ref[...]), nx, rxr.at[1], rxs.at[1])
+    send_rewards("gx", 0, 0, rxs, rxr)
     send_rewards("gx", 0, 1, rxs, rxr)
     fetches[2].wait()
     len_row = jnp.concatenate([len_ref[t : t + 1, :] for t in range(rows // LANES)], axis=1)
@@ -205,7 +210,7 @@
         both = jnp.concatenate(
             [jnp.where(low(), penalty, other), jnp.where(low(), other, penalty)], axis=1
         )
-        got = pick(hot1[...], both, 2)
+        got = pick(hot1[...], both)
         for h in range(2):
             part = got[:, h * LANES : (h + 1) * LANES]
             xr[2 * c + h, 0:cx, :] = part[0:cx, :]
@@ -214,17 +219,17 @@
                 at = pl.ds(k * cx, cx)
                 send(
                     "gx", k, xs.at[2 * c + h, at], xr.at[2 * c + h, at],
-                    xsend.at[2 * c + h], xrecv.at[2 * c + h],
+                    xsend, xrecv.at[2 * c + h],
                 )
 
     def to_y(c):
         drain(xr.at[c, pl.ds(cx, slots - cx)], xrecv.at[c])
-        got = pick(hot2[...], xr[c], 2)
+        got = pick(hot2[...], xr[c])
         yr[c, 0:cy, :] = got[0:cy, :]
         ys[c] = got
         for k in far_first(ny):
             at = pl.ds(k * cy, cy)
-            send("gy", k, ys.at[c, at], yr.at[c, at], ysend.at[c], yrecv.at[c])
+            send("gy", k, ys.at[c, at], yr.at[c, at], ysend, yrecv.at[c])
 
     def drain_y(c):
         drain(yr.at[c, pl.ds(cy, slots - cy)], yrecv.at[c])
@@ -232,7 +237,7 @@
     def gather_z(c):
         drain_y(2 * c)
         drain_y(2 * c + 1)
-        return pick(hot3[...], jnp.concatenate([yr[2 * c], yr[2 * c + 1]], axis=1), 2)
+        return pick(hot3[...], jnp.concatenate([yr[2 * c], yr[2 * c + 1]], axis=1))
 
     def loss(even, odd, weights):
         return jnp.where(low(), even, odd) - weights * swap(jnp.where(low(), odd, even))
@@ -242,15 +247,15 @@
         zs[c] = rows_out
         for k in far_first(nz):
             at = pl.ds(k * cz, cz)
-            send("gz", k, zs.at[c, at], zr.at[c, at], zsend.at[c], zrecv.at[c])
+            send("gz", k, zs.at[c, at], zr.at[c, at], zsend, zrecv.at[c])
 
     to_x(0)
 
     drain(hxr.at[pl.ds(1, nx - 1)], hrecv.at[0])
     head = jnp.concatenate([hxr[k] for k in range(nx)], axis=1)
     held = head.astype(jnp.int32)
-    hot2[...] = one_hot(slots_of(held[0:1, :], held[3:4, :] > 0, my, ny, cy), slots)
-    head = carry(head, hot2[...])
+    hot2[...] = one_hot(slots_of((held - 1) >> log2(rows * nz), held > 0, my, ny, cy), slots)
+    head = carry(held, hot2[...])
     hyr[0] = head[:, 0:cy]
     for k in range(1, ny):
         hys[k] = head[:, k * cy : (k + 1) * cy]
@@ -258,7 +263,7 @@
         send("gy", k, hys.at[k], hyr.at[k], hsend.at[1], hrecv.at[1])
 
     for half in range(2):
-        drain_rewards(0, half, rxr, rrecv)
+        drain_rewards(0, half, rxr)
         spread_rewards(hot2[...], unpacked(rxr.at[half]), ny, ryr.at[half], rys.at[half])
         send_rewards("gy", 1, half, rys, ryr)
 
@@ -267,8 +272,10 @@
     drain(hyr.at[pl.ds(1, ny - 1)], hrecv.at[1])
     head = jnp.concatenate([hyr[k] for k in range(ny)], axis=1)
     held = head.astype(jnp.int32)
-    hot3[...] = one_hot(slots_of(held[1:2, :], held[3:4, :] > 0, mz, nz, cz), slots)
-    head = carry(head, hot3[...])
+    hot3[...] = one_hot(
+        slots_of(((held - 1) >> log2(rows)) & (nz - 1), held > 0, mz, nz, cz), slots
+    )
+    head = carry(held, hot3[...])
     hzr[0] = head[:, 0:LANES]
     for t in range(tiles):
         hzs[t] = head[:, t * LANES : (t + 1) * LANES]
@@ -276,7 +283,7 @@
         send("gz", k, hzs.at[k // per_tile], hzr.at[k], hsend.at[2], hrecv.at[2])
 
     def rewards_to_z(half):
-        drain_rewards(1, half, ryr, rrecv)
+        drain_rewards(1, half, ryr)
         spread_rewards(hot3[...], unpacked(ryr.at[half]), nz, rzr.at[half], rzs.at[half])
         send_rewards("gz", 2, half, rzs, rzr)
 
@@ -284,26 +291,23 @@
     to_y(0)
     rewards_to_z(1)
     to_x(2)
-    drain(hzr.at[pl.ds(1, nz - 1)], hrecv.at[2])
-    held = along_slots(lambda k: hzr[k]).astype(jnp.int32)
-    place = jnp.where(held[3:4, :] > 0, held[2:3, :], -1)
-    hot4[...] = jnp.where(iota((rows, slots), 0) == place, 1.0, 0.0).astype(BF16)
     to_y(1)
     to_x(3)
     fetches[5].wait()
 
     drain_y(0)
-    send_z(0, pick(hot3[...], yr[0], 2))
+    send_z(0, pick(hot3[...], yr[0]))
     to_y(2)
-    to_x(4)
+    drain(hzr.at[pl.ds(1, nz - 1)], hrecv.at[2])
+    held = along_slots(lambda k: hzr[k]).astype(jnp.int32)
+    place = jnp.where(held > 0, (held - 1) & (rows - 1), -1)
+    hot4[...] = jnp.where(iota((rows, slots), 0) == place, 1.0, 0.0).astype(BF16)
     to_y(3)
-    drain_y(1)
-    zg[...] = pick(hot3[...], yr[1], 2)
-
-    drain_rewards(2, 0, rzr, rrecv)
-    judged = pick(hot4[...], unpacked(rzr.at[0]), 3)
-    drain_rewards(2, 1, rzr, rrecv)
-    judged = jnp.where(low(), judged, swap(pick(hot4[...], unpacked(rzr.at[1]), 3)))
+
+    drain_rewards(2, 0, rzr)
+    judged = pick_half(hot4[...], unpacked(rzr.at[0]))
+    drain_rewards(2, 1, rzr)
+    judged = jnp.where(low(), judged, swap(pick_half(hot4[...], unpacked(rzr.at[1]))))
     grouped = judged.reshape(rows // GROUP, GROUP, LANES)
     centre = jnp.mean(grouped, axis=1, keepdims=True)
     deviation = grouped - centre
@@ -311,13 +315,15 @@
     advantages = (deviation / jnp.sqrt(spread + 1.0)).reshape(rows, LANES)
     weight = jnp.sum(advantages * mix_ref[...], axis=1, keepdims=True)
     row = jnp.sum(hot4[...].astype(F32) * weight, axis=0, keepdims=True)
-    wr[0] = jnp.broadcast_to(row[:, 0:LANES], (HEAD, LANES))
+    wr[0] = row[:, 0:LANES]
     for t in range(tiles):
-        ws[t] = jnp.broadcast_to(row[:, t * LANES : (t + 1) * LANES], (HEAD, LANES))
+        ws[t] = row[:, t * LANES : (t + 1) * LANES]
     for k in far_first(nz):
-        send("gz", -k, ws.at[k // per_tile], wr.at[k], rsend.at[6], rrecv.at[6])
-    send_z(chunks, zg[...])
+        send("gz", -k, ws.at[k // per_tile], wr.at[k], rsend.at[3], rrecv.at[6])
+    drain_y(1)
+    send_z(chunks, pick(hot3[...], yr[1]))
     adv_ref[...] = advantages
+    to_x(4)
     wrow[...] = jnp.broadcast_to(weight, (rows, LANES))
 
     to_y(4)
@@ -326,7 +332,7 @@
     second = gather_z(1)
     to_y(6)
     drain(wr.at[pl.ds(1, nz - 1)], rrecv.at[6])
-    wcol[...] = jnp.broadcast_to(to_column(along_slots(lambda k: wr[k])[0:1, :]), (slots, LANES))
+    wcol[...] = jnp.broadcast_to(to_column(along_slots(lambda k: wr[k])), (slots, LANES))
     send_z(1, loss(second[:, 0:LANES], second[:, LANES:], wcol[...]))
     to_x(6)
     to_y(7)
@@ -348,30 +354,39 @@
 
     for i, (h, r, n) in enumerate(((hxr, rxr, nx), (hyr, ryr, ny), (hzr, rzr, nz))):
         drain(h.at[pl.ds(1, n - 1)], hsend.at[i])
-        drain_rewards(i, 0, r, rsend)
-        drain_rewards(i, 1, r, rsend)
-    drain(wr.at[pl.ds(1, nz - 1)], rsend.at[6])
-
-    @pl.loop(0, 2 * chunks)
-    def _(c):
-        drain(xs.at[c, pl.ds(cx, slots - cx)], xsend.at[c])
-        drain(ys.at[c, pl.ds(cy, slots - cy)], ysend.at[c])
+        drain(r.at[:, pl.ds(1, n - 1)], rsend.at[i])
+    drain(wr.at[pl.ds(1, nz - 1)], rsend.at[3])
+    drain(xs.at[:, pl.ds(cx, slots - cx)], xsend)
+    drain(ys.at[:, pl.ds(cy, slots - cy)], ysend)
 
     def arrived(c):
         drain(zr.at[c, pl.ds(cz, slots - cz)], zrecv.at[c])
-        return pick(hot4[...], zr[c], 2)
+        return pick(hot4[...], zr[c])
 
     even = arrived(0)
     tok_ref[:, 0:LANES] = loss(even, arrived(chunks), wrow[...])
 
-    @pl.loop(1, chunks)
-    def _(c):
+    def finish(c):
         columns = pl.ds(pl.multiple_of(c * LANES, LANES), LANES)
         tok_ref[:, columns] = arrived(c)
 
-    @pl.loop(0, chunks + 1)
+    @pl.loop(1, chunks - 1)
     def _(c):
-        drain(zs.at[c, pl.ds(cz, slots - cz)], zsend.at[c])
+        finish(c)
+
+    drain(zs.at[:, pl.ds(cz, slots - cz)], zsend)
+    finish(chunks - 1)
+
+
+def store(tok_ref, adv_ref, tok_hbm, adv_hbm, sems):
+    copies = [
+        pltpu.make_async_copy(tok_ref, tok_hbm, sems.at[0]),
+        pltpu.make_async_copy(adv_ref, adv_hbm, sems.at[1]),
+    ]
+    for copy in copies:
+        copy.start()
+    for copy in copies:
+        copy.wait()
 
 
 def on_device(sizes, log_probs, ref_log_probs, rewards, destination, lengths, mixing):
@@ -384,12 +399,12 @@
     sem = pltpu.SemaphoreType.DMA
 
     def head_buffer(n):
-        return pltpu.VMEM((n, HEAD, LANES), F32)
+        return pltpu.VMEM((n, 1, LANES), F32)
 
     def reward_buffer(n):
         return pltpu.VMEM((2, n, slots // n // 2, LANES), F32)
 
-    return pl.pallas_call(
+    token_loss, advantages = pl.pallas_call(
         functools.partial(kernel, sizes, chunks),
         out_shape=(pltpu.VMEM((rows, width), F32), pltpu.VMEM((rows, LANES), F32)),
         in_specs=[pl.BlockSpec(memory_space=pl.ANY)] * 6,
@@ -416,9 +431,9 @@
             reward_buffer(nx), reward_buffer(nx),
             reward_buffer(ny), reward_buffer(ny),
             reward_buffer(nz), reward_buffer(nz),
-            wide, wide, wide, wide, pltpu.VMEM((slots, LANES), F32), thin, thin,
-            sem((6,)), sem((3,)), sem((3,)), sem((7,)), sem((7,)),
-            sem((2 * chunks,)), sem((2 * chunks,)), sem((2 * chunks,)), sem((2 * chunks,)), sem((chunks + 1,)), sem((chunks + 1,)),
+            wide, wide, wide, wide, thin, thin,
+            sem((6,)), sem((3,)), sem((3,)), sem((4,)), sem((7,)),
+            sem, sem((2 * chunks,)), sem, sem((2 * chunks,)), sem, sem((chunks + 1,)),
         ],
         compiler_params=pltpu.CompilerParams(
             collective_id=0, has_side_effects=True, vmem_limit_bytes=60 << 20
@@ -432,6 +447,20 @@
         ref_log_probs,
         rewards,
     )
+    return pl.pallas_call(
+        store,
+        out_shape=(
+            jax.ShapeDtypeStruct((rows, width), F32),
+            jax.ShapeDtypeStruct((rows, LANES), F32),
+        ),
+        in_specs=[pl.BlockSpec(memory_space=pltpu.VMEM)] * 2,
+        out_specs=(pl.BlockSpec(memory_space=pl.ANY),) * 2,
+        scratch_shapes=[sem((2,))],
+        name="store",
+    )(
+        pltpu.with_memory_space_constraint(token_loss, pltpu.VMEM),
+        pltpu.with_memory_space_constraint(advantages, pltpu.VMEM),
+    )
 
 
 def solution(mesh):

time: 85.3 us -> 81 us (0.950)
  Pallas kernels: 82.9 us -> 80.3 us
  local copies, waits for them, and re-layouts: 1.63 us -> 0 us
    pallas_call x1, Pallas kernels: 82.9 us -> 79.3 us  [on_device(): pl.pallas_call(functools.partial(kernel, sizes, chunks), out_shape=(pltpu...]
    unnamed x2 -> x0, local copies, waits for them, and re-layouts: 1.63 us -> none
    pallas_call x0 -> x1, Pallas kernels: none -> 1.02 us  [on_device(): pl.pallas_call(store, out_shape=(jax.ShapeDtypeStruct((rows, width), F32)...]
where the time goes in v3:
time: 81 us; the launch traced here: 80.9 us
  Pallas kernels  80.3 us (99%)
    pallas_call x1, Pallas kernels, on_device(): pl.pallas_call(functools.partial(kernel, sizes, chunks), out_shape=(pltpu...  79.3 us

profile of v3, /device:TPU:1, one launch (start us, length us, event | category | flops | bytes accessed | tf_op | source)
XLA Modules:
  0.0 80.9 jit_solution(13270156468904803185)
XLA Ops:
  0.6 79.3 %regroup.1 = (f32[256,1024]{1,0:T(8,128)S(1)}, f32[256,128]{1,0:T(8,128)S(1)}) custom-call(s32[2,128]{1,0:T(2,128)} %bitcast.3, s32[2,128]{1,0:T(2,128)} %bitcast.4, f32[1,128]{1,0:T(1,128)} %bitcast.5, f32[256,1024]{1,0:T(8,128)} %lp_hbm.1, f32[256,1024]{1,0:T(8,128)} %rp_hbm.1, f32[256,128]{1,0:T(8,128)} %rw_hbm.1), custom_call_target="tpu_custom_call" | custom-call | tf_op jit(solution)/shard_map/regroup/pallas_call | solution.py:407
  79.9 1.0 %store.1 = (f32[256,1024]{1,0:T(8,128)}, f32[256,128]{1,0:T(8,128)}) custom-call(f32[256,1024]{1,0:T(8,128)S(1)} %get-tuple-element.4.tok_ref, f32[256,128]{1,0:T(8,128)S(1)} %get-tuple-element.5.adv_ref), custom_call_target="tpu_custom_call" | custom-call | tf_op jit(solution)/shard_map/store/pallas_call | solution.py:450

commit v4 on v3

--- a/solution.py
+++ b/solution.py
@@ -74,7 +74,7 @@
     hxs, hxr, hys, hyr, hzs, hzr, ws, wr,
     rxs, rxr, rys, ryr, rzs, rzr,
     xs, xr, ys, yr, zs, zr,
-    loads, hsend, hrecv, rsend, rrecv, xsend, xrecv, ysend, yrecv, zsend, zrecv,
+    loads, hsend, hrecv, rsend, rrecv, xsend, xrecv, ysend, yrecv, nsend, zsend, zrecv,
 ):
     nx, ny, nz = sizes
     rows = lp_ref.shape[0]
@@ -88,6 +88,9 @@
     def far_first(n):
         return sorted(range(1, n), key=lambda k: -min(k, n - k))
 
+    near = [k for k in far_first(nz) if min(k, nz - k) <= 3]
+    far = [k for k in far_first(nz) if k not in near]
+
     def peer(axis, step):
         me, n = ring[axis]
         return {axis: lax.rem(me + (step + n), n)}
@@ -101,13 +104,13 @@
             )
         )
     ]
+    barrier = pltpu.get_barrier_semaphore()
+    for axis in ("gz", "gx", "gy"):
+        for k in far_first(ring[axis][1]):
+            pl.semaphore_signal(barrier, inc=1, device_id=peer(axis, k), device_id_type=MESH)
+
     for fetch in fetches:
         fetch.start()
-
-    barrier = pltpu.get_barrier_semaphore()
-    for axis in ("gz", "gx", "gy"):
-        for k in range(1, ring[axis][1]):
-            pl.semaphore_signal(barrier, inc=1, device_id=peer(axis, k), device_id_type=MESH)
 
     def send(axis, k, src, dst, ssem, rsem):
         pltpu.make_async_remote_copy(
@@ -239,6 +242,11 @@
         drain_y(2 * c + 1)
         return pick(hot3[...], jnp.concatenate([yr[2 * c], yr[2 * c + 1]], axis=1))
 
+    def send_some(c, peers, sem_at):
+        for k in peers:
+            at = pl.ds(k * cz, cz)
+            send("gz", k, zs.at[c, at], zr.at[c, at], nsend.at[sem_at], zrecv.at[c])
+
     def loss(even, odd, weights):
         return jnp.where(low(), even, odd) - weights * swap(jnp.where(low(), odd, even))
 
@@ -266,8 +274,6 @@
         drain_rewards(0, half, rxr)
         spread_rewards(hot2[...], unpacked(rxr.at[half]), ny, ryr.at[half], rys.at[half])
         send_rewards("gy", 1, half, rys, ryr)
-
-    to_x(1)
 
     drain(hyr.at[pl.ds(1, ny - 1)], hrecv.at[1])
     head = jnp.concatenate([hyr[k] for k in range(ny)], axis=1)
@@ -282,6 +288,8 @@
     for k in far_first(nz):
         send("gz", k, hzs.at[k // per_tile], hzr.at[k], hsend.at[2], hrecv.at[2])
 
+    to_x(1)
+
     def rewards_to_z(half):
         drain_rewards(1, half, ryr)
         spread_rewards(hot3[...], unpacked(ryr.at[half]), nz, rzr.at[half], rzs.at[half])
@@ -296,7 +304,8 @@
     fetches[5].wait()
 
     drain_y(0)
-    send_z(0, pick(hot3[...], yr[0]))
+    zs[0] = pick(hot3[...], yr[0])
+    send_some(0, far, 0)
     to_y(2)
     drain(hzr.at[pl.ds(1, nz - 1)], hrecv.at[2])
     held = along_slots(lambda k: hzr[k]).astype(jnp.int32)
@@ -319,24 +328,40 @@
     for t in range(tiles):
         ws[t] = row[:, t * LANES : (t + 1) * LANES]
     for k in far_first(nz):
-        send("gz", -k, ws.at[k // per_tile], wr.at[k], rsend.at[3], rrecv.at[6])
+        came = rrecv.at[6] if k in near else rrecv.at[7]
+        send("gz", -k, ws.at[k // per_tile], wr.at[k], rsend.at[3], came)
+
     drain_y(1)
-    send_z(chunks, pick(hot3[...], yr[1]))
+    zs[chunks] = pick(hot3[...], yr[1])
+    send_some(chunks, far, 1)
     adv_ref[...] = advantages
+    wrow[...] = jnp.broadcast_to(weight, (rows, LANES))
     to_x(4)
-    wrow[...] = jnp.broadcast_to(weight, (rows, LANES))
-
     to_y(4)
     to_x(5)
+
+    drain(wr.at[pl.ds(0, len(near))], rrecv.at[6])
+    none = jnp.zeros((1, LANES), F32)
+    weights = to_column(along_slots(lambda k: none if k in far else wr[k]))
+    first = loss(zs[0], zs[chunks], weights)
+    zr[chunks + 1, 0:cz, :] = first[0:cz, :]
+    zs[chunks + 1] = first
+    send_some(chunks + 1, near, 2)
     to_y(5)
     second = gather_z(1)
-    to_y(6)
-    drain(wr.at[pl.ds(1, nz - 1)], rrecv.at[6])
+    drain(wr.at[pl.ds(0, len(far))], rrecv.at[7])
     wcol[...] = jnp.broadcast_to(to_column(along_slots(lambda k: wr[k])), (slots, LANES))
     send_z(1, loss(second[:, 0:LANES], second[:, LANES:], wcol[...]))
+    to_y(6)
     to_x(6)
     to_y(7)
     to_x(7)
+
+    low_far, high_far = min(far) * cz, (max(far) + 1) * cz
+    for c in (0, chunks):
+        zr[c, 0:low_far, :] = jnp.zeros((low_far, LANES), F32)
+        zr[c, high_far:slots, :] = jnp.zeros((slots - high_far, LANES), F32)
+    zr[chunks + 1, low_far:high_far, :] = jnp.zeros((high_far - low_far, LANES), F32)
 
     def loss_to_z(c):
         got = gather_z(c)
@@ -359,13 +384,15 @@
     drain(xs.at[:, pl.ds(cx, slots - cx)], xsend)
     drain(ys.at[:, pl.ds(cy, slots - cy)], ysend)
 
+    for c, peers in ((0, far), (chunks, far), (chunks + 1, near)):
+        drain(zr.at[c, pl.ds(0, len(peers) * cz)], zrecv.at[c])
+    first = loss(pick(hot4[...], zr[0]), pick(hot4[...], zr[chunks]), wrow[...])
+    tok_ref[:, 0:LANES] = first + pick(hot4[...], zr[chunks + 1])
+
     def arrived(c):
         drain(zr.at[c, pl.ds(cz, slots - cz)], zrecv.at[c])
         return pick(hot4[...], zr[c])
 
-    even = arrived(0)
-    tok_ref[:, 0:LANES] = loss(even, arrived(chunks), wrow[...])
-
     def finish(c):
         columns = pl.ds(pl.multiple_of(c * LANES, LANES), LANES)
         tok_ref[:, columns] = arrived(c)
@@ -374,7 +401,9 @@
     def _(c):
         finish(c)
 
-    drain(zs.at[:, pl.ds(cz, slots - cz)], zsend)
+    for i, peers in enumerate((far, far, near)):
+        drain(zs.at[0, pl.ds(0, len(peers) * cz)], nsend.at[i])
+    drain(zs.at[pl.ds(1, chunks - 1), pl.ds(cz, slots - cz)], zsend)
     finish(chunks - 1)
 
 
@@ -395,7 +424,7 @@
     chunks = width // LANES
     nx, ny, nz = sizes
     wide = pltpu.VMEM((2 * chunks, slots, LANES), F32)
-    thin = pltpu.VMEM((chunks + 1, slots, LANES), F32)
+    thin = pltpu.VMEM((chunks + 2, slots, LANES), F32)
     sem = pltpu.SemaphoreType.DMA
 
     def head_buffer(n):
@@ -432,8 +461,8 @@
             reward_buffer(ny), reward_buffer(ny),
             reward_buffer(nz), reward_buffer(nz),
             wide, wide, wide, wide, thin, thin,
-            sem((6,)), sem((3,)), sem((3,)), sem((4,)), sem((7,)),
-            sem, sem((2 * chunks,)), sem, sem((2 * chunks,)), sem, sem((chunks + 1,)),
+            sem((6,)), sem((3,)), sem((3,)), sem((4,)), sem((8,)),
+            sem, sem((2 * chunks,)), sem, sem((2 * chunks,)), sem((3,)), sem, sem((chunks + 2,)),
         ],
         compiler_params=pltpu.CompilerParams(
             collective_id=0, has_side_effects=True, vmem_limit_bytes=60 << 20

time: 81 us -> 80.1 us (0.989)
  Pallas kernels: 80.3 us -> 79.4 us
    pallas_call x1, Pallas kernels: 79.3 us -> 78.4 us  [on_device(): pl.pallas_call(functools.partial(kernel, sizes, chunks), out_shape=(pltpu...]
where the time goes in v4:
time: 80.1 us; the launch traced here: 80 us
  Pallas kernels  79.4 us (99%)
    pallas_call x1, Pallas kernels, on_device(): pl.pallas_call(functools.partial(kernel, sizes, chunks), out_shape=(pltpu...  78.4 us

profile of v4, /device:TPU:1, one launch (start us, length us, event | category | flops | bytes accessed | tf_op | source)
XLA Modules:
  0.0 80.0 jit_solution(17409186993426399612)
XLA Ops:
  0.6 78.4 %regroup.1 = (f32[256,1024]{1,0:T(8,128)S(1)}, f32[256,128]{1,0:T(8,128)S(1)}) custom-call(s32[2,128]{1,0:T(2,128)} %bitcast.3, s32[2,128]{1,0:T(2,128)} %bitcast.4, f32[1,128]{1,0:T(1,128)} %bitcast.5, f32[256,1024]{1,0:T(8,128)} %lp_hbm.1, f32[256,1024]{1,0:T(8,128)} %rp_hbm.1, f32[256,128]{1,0:T(8,128)} %rw_hbm.1), custom_call_target="tpu_custom_call" | custom-call | tf_op jit(solution)/shard_map/regroup/pallas_call | solution.py:436
  79.0 1.0 %store.1 = (f32[256,1024]{1,0:T(8,128)}, f32[256,128]{1,0:T(8,128)}) custom-call(f32[256,1024]{1,0:T(8,128)S(1)} %get-tuple-element.4.tok_ref, f32[256,128]{1,0:T(8,128)S(1)} %get-tuple-element.5.adv_ref), custom_call_target="tpu_custom_call" | custom-call | tf_op jit(solution)/shard_map/store/pallas_call | solution.py:479

commit v5 on v4

--- a/solution.py
+++ b/solution.py
@@ -86,7 +86,7 @@
     ring = {"gx": (mx, nx), "gy": (my, ny), "gz": (mz, nz)}
 
     def far_first(n):
-        return sorted(range(1, n), key=lambda k: -min(k, n - k))
+        return [1, 3, 2] if n == 4 else sorted(range(1, n), key=lambda k: -min(k, n - k))
 
     near = [k for k in far_first(nz) if min(k, nz - k) <= 3]
     far = [k for k in far_first(nz) if k not in near]
@@ -225,21 +225,17 @@
                     xsend, xrecv.at[2 * c + h],
                 )
 
-    def to_y(c):
+    def to_y(c, pair):
         drain(xr.at[c, pl.ds(cx, slots - cx)], xrecv.at[c])
         got = pick(hot2[...], xr[c])
         yr[c, 0:cy, :] = got[0:cy, :]
         ys[c] = got
         for k in far_first(ny):
             at = pl.ds(k * cy, cy)
-            send("gy", k, ys.at[c, at], yr.at[c, at], ysend, yrecv.at[c])
-
-    def drain_y(c):
-        drain(yr.at[c, pl.ds(cy, slots - cy)], yrecv.at[c])
+            send("gy", k, ys.at[c, at], yr.at[c, at], ysend, yrecv.at[pair])
 
     def gather_z(c):
-        drain_y(2 * c)
-        drain_y(2 * c + 1)
+        drain(yr.at[pl.ds(2 * c, 2), pl.ds(cy, slots - cy)], yrecv.at[c])
         return pick(hot3[...], jnp.concatenate([yr[2 * c], yr[2 * c + 1]], axis=1))
 
     def send_some(c, peers, sem_at):
@@ -296,22 +292,22 @@
         send_rewards("gz", 2, half, rzs, rzr)
 
     rewards_to_z(0)
-    to_y(0)
+    to_y(0, 0)
     rewards_to_z(1)
     to_x(2)
-    to_y(1)
+    to_y(1, chunks)
     to_x(3)
     fetches[5].wait()
 
-    drain_y(0)
+    drain(yr.at[0, pl.ds(cy, slots - cy)], yrecv.at[0])
     zs[0] = pick(hot3[...], yr[0])
     send_some(0, far, 0)
-    to_y(2)
+    to_y(2, 1)
     drain(hzr.at[pl.ds(1, nz - 1)], hrecv.at[2])
     held = along_slots(lambda k: hzr[k]).astype(jnp.int32)
     place = jnp.where(held > 0, (held - 1) & (rows - 1), -1)
     hot4[...] = jnp.where(iota((rows, slots), 0) == place, 1.0, 0.0).astype(BF16)
-    to_y(3)
+    to_y(3, 1)
 
     drain_rewards(2, 0, rzr)
     judged = pick_half(hot4[...], unpacked(rzr.at[0]))
@@ -331,13 +327,13 @@
         came = rrecv.at[6] if k in near else rrecv.at[7]
         send("gz", -k, ws.at[k // per_tile], wr.at[k], rsend.at[3], came)
 
-    drain_y(1)
+    drain(yr.at[1, pl.ds(cy, slots - cy)], yrecv.at[chunks])
     zs[chunks] = pick(hot3[...], yr[1])
     send_some(chunks, far, 1)
     adv_ref[...] = advantages
     wrow[...] = jnp.broadcast_to(weight, (rows, LANES))
     to_x(4)
-    to_y(4)
+    to_y(4, 2)
     to_x(5)
 
     drain(wr.at[pl.ds(0, len(near))], rrecv.at[6])
@@ -347,14 +343,14 @@
     zr[chunks + 1, 0:cz, :] = first[0:cz, :]
     zs[chunks + 1] = first
     send_some(chunks + 1, near, 2)
-    to_y(5)
+    to_y(5, 2)
     second = gather_z(1)
     drain(wr.at[pl.ds(0, len(far))], rrecv.at[7])
     wcol[...] = jnp.broadcast_to(to_column(along_slots(lambda k: wr[k])), (slots, LANES))
     send_z(1, loss(second[:, 0:LANES], second[:, LANES:], wcol[...]))
-    to_y(6)
+    to_y(6, 3)
     to_x(6)
-    to_y(7)
+    to_y(7, 3)
     to_x(7)
 
     low_far, high_far = min(far) * cz, (max(far) + 1) * cz
@@ -370,8 +366,8 @@
     @pl.loop(2, chunks - 2)
     def _(c):
         loss_to_z(c)
-        to_y(2 * c + 4)
-        to_y(2 * c + 5)
+        to_y(2 * c + 4, c + 2)
+        to_y(2 * c + 5, c + 2)
 
     @pl.loop(chunks - 2, chunks)
     def _(c):
@@ -462,7 +458,7 @@
             reward_buffer(nz), reward_buffer(nz),
             wide, wide, wide, wide, thin, thin,
             sem((6,)), sem((3,)), sem((3,)), sem((4,)), sem((8,)),
-            sem, sem((2 * chunks,)), sem, sem((2 * chunks,)), sem((3,)), sem, sem((chunks + 2,)),
+            sem, sem((2 * chunks,)), sem, sem((chunks + 1,)), sem((3,)), sem, sem((chunks + 2,)),
         ],
         compiler_params=pltpu.CompilerParams(
             collective_id=0, has_side_effects=True, vmem_limit_bytes=60 << 20

time: 80.1 us -> 79.9 us (level)
  no operation moved by 1% of the time
where the time goes in v5:
time: 79.9 us
  Pallas kernels  79.2 us (99%)
    pallas_call x1, Pallas kernels, on_device(): pl.pallas_call(functools.partial(kernel, sizes, chunks), out_shape=(pltpu...  78.2 us

profile of v5, /device:TPU:1, one launch (start us, length us, event | category | flops | bytes accessed | tf_op | source)
XLA Modules:
  0.0 79.9 jit_solution(16647749226743770513)
XLA Ops:
  0.6 78.2 %regroup.1 = (f32[256,1024]{1,0:T(8,128)S(1)}, f32[256,128]{1,0:T(8,128)S(1)}) custom-call(s32[2,128]{1,0:T(2,128)} %bitcast.3, s32[2,128]{1,0:T(2,128)} %bitcast.4, f32[1,128]{1,0:T(1,128)} %bitcast.5, f32[256,1024]{1,0:T(8,128)} %lp_hbm.1, f32[256,1024]{1,0:T(8,128)} %rp_hbm.1, f32[256,128]{1,0:T(8,128)} %rw_hbm.1), custom_call_target="tpu_custom_call" | custom-call | tf_op jit(solution)/shard_map/regroup/pallas_call | solution.py:432
  78.8 1.0 %store.1 = (f32[256,1024]{1,0:T(8,128)}, f32[256,128]{1,0:T(8,128)}) custom-call(f32[256,1024]{1,0:T(8,128)S(1)} %get-tuple-element.4.tok_ref, f32[256,128]{1,0:T(8,128)S(1)} %get-tuple-element.5.adv_ref), custom_call_target="tpu_custom_call" | custom-call | tf_op jit(solution)/shard_map/store/pallas_call | solution.py:475

commit v6 on v5

--- a/solution.py
+++ b/solution.py
@@ -47,12 +47,8 @@
 
 def pick_half(onehot, x):
     first = x.astype(BF16).astype(F32)
-    rest = x - first
-    second = rest.astype(BF16).astype(F32)
-    third = (rest - second).astype(BF16)
-    both = jnp.where(low(), first, swap(second)).astype(BF16)
-    got = dot(onehot, jnp.concatenate([both, third], axis=1))
-    return (got[:, 0:LANES] + swap(got[:, 0:LANES])) + got[:, LANES:]
+    got = dot(onehot, jnp.where(low(), first, swap(x - first)).astype(BF16))
+    return got + swap(got)
 
 
 def to_column(row):

time: 79.9 us -> 80.3 us (level)
  no operation moved by 1% of the time
where the time goes in v6:
time: 80.3 us; the launch traced here: 80.2 us
  Pallas kernels  79.5 us (99%)
    pallas_call x1, Pallas kernels, on_device(): pl.pallas_call(functools.partial(kernel, sizes, chunks), out_shape=(pltpu...  78.5 us

profile of v6, /device:TPU:1, one launch (start us, length us, event | category | flops | bytes accessed | tf_op | source)
XLA Modules:
  0.0 80.2 jit_solution(9388339443574957232)
XLA Ops:
  0.6 78.5 %regroup.1 = (f32[256,1024]{1,0:T(8,128)S(1)}, f32[256,128]{1,0:T(8,128)S(1)}) custom-call(s32[2,128]{1,0:T(2,128)} %bitcast.3, s32[2,128]{1,0:T(2,128)} %bitcast.4, f32[1,128]{1,0:T(1,128)} %bitcast.5, f32[256,1024]{1,0:T(8,128)} %lp_hbm.1, f32[256,1024]{1,0:T(8,128)} %rp_hbm.1, f32[256,128]{1,0:T(8,128)} %rw_hbm.1), custom_call_target="tpu_custom_call" | custom-call | tf_op jit(solution)/shard_map/regroup/pallas_call | solution.py:428
  79.1 1.0 %store.1 = (f32[256,1024]{1,0:T(8,128)}, f32[256,128]{1,0:T(8,128)}) custom-call(f32[256,1024]{1,0:T(8,128)S(1)} %get-tuple-element.4.tok_ref, f32[256,128]{1,0:T(8,128)S(1)} %get-tuple-element.5.adv_ref), custom_call_target="tpu_custom_call" | custom-call | tf_op jit(solution)/shard_map/store/pallas_call | solution.py:471
